TPU v7x, 32 devices: a whole 2x2x4 slice. The times are simulated.
32 devices in a mesh: gx: 4 (over y, x), gy: 8 (over z, core).
Axes of the slice: x: 2, y: 2, z: 4, core: 2. Of those that a mesh axis runs over, the one named last changes fastest.
Arguments:
- replay_deter: float32 [8192, 2048], P(('gx', 'gy')), may hold values from -1 to 1
- replay_stoch: int32 [8192, 32], P(('gx', 'gy')), may hold values from 0 to 31
- send_rows: int32 [1024, 8], P(('gx', 'gy')), may hold values from 0 to 255
- send_counts: int32 [32, 32], P(('gx', 'gy')), may hold values from 0 to 8, as said below
- actions: int32 [8192, 4], P(('gx', 'gy')), may hold values from 0 to 17
- samples: int32 [8192, 4, 32], P(('gx', 'gy')), may hold values from 0 to 31
- w_stoch: bfloat16 [1024, 6144], P('gy'), may hold values from -1 to 1
- w_deter: bfloat16 [4, 512, 1536], P(None, 'gy'), may hold values from -0.25 to 0.25
- act_table: bfloat16 [18, 6144], replicated, may hold values from -3 to 3
- w_prior: bfloat16 [2048, 1024], P('gy'), may hold values from -0.037353516 to 0.037353516
Outputs:
- imagined: bfloat16 [8192, 4, 2048], P(('gx', 'gy'))
- log_prob: float32 [8192, 4, 32], P(('gx', 'gy'))
Inputs may be any that keep to these rules, and one draw needn't show every extreme that they name: `send_rows`: entries past a destination's count are unused. `send_counts`: each source's counts sum to exactly 128; every source sends 8 rows to some owner, and some owner receives 8 rows from every source.
All inputs are finite; a program needn't handle non-finite values.
Results may differ from a plain program's by a relative error of at most 0.0022.
Values may be sent and summed in bfloat16 or wider, within the bound.
No kernel may reach another device: no remote copies, remote signals or barrier semaphores. Data moves between devices by JAX's collectives and lax.ppermute only.
A program may use at most 128 MiB of HBM per device.

v0:
```python
import jax
import jax.numpy as jnp
from jax import lax
from jax.sharding import PartitionSpec as P

GROUPS = 32
CLASSES = 32
STEPS = 4


def gate_inputs(stoch, action, actions_count):
    rows = stoch.shape[0]
    onehot = (
        (stoch[:, :, None] == jnp.arange(CLASSES, dtype=jnp.int32)[None, None, :])
        .reshape(rows, GROUPS * CLASSES)
        .astype(jnp.bfloat16)
    )
    act_hot = (action[:, None] == jnp.arange(actions_count, dtype=jnp.int32)[None, :]).astype(
        jnp.bfloat16
    )
    return (onehot, act_hot)


def imagine(start, first, acts, samps, stoch_full, deter_full, act_table):
    blocks = deter_full.shape[0]
    width = deter_full.shape[1]
    pieces = [start[:, b * width : (b + 1) * width] for b in range(blocks)]
    stoch = first
    states = []
    for step in range(STEPS):
        onehot, act_hot = gate_inputs(stoch, acts[:, step], act_table.shape[0])
        input_term = jnp.dot(onehot, stoch_full, preferred_element_type=jnp.float32) + jnp.dot(
            act_hot, act_table, preferred_element_type=jnp.float32
        )
        fresh = []
        for b in range(blocks):
            before = pieces[b]
            gates = input_term[:, 3 * width * b : 3 * width * (b + 1)] + jnp.dot(
                before.astype(jnp.bfloat16), deter_full[b], preferred_element_type=jnp.float32
            )
            reset = jax.nn.sigmoid(gates[:, :width])
            cand = jnp.tanh(reset * gates[:, width : 2 * width])
            update = jax.nn.sigmoid(gates[:, 2 * width :] - 1.0)
            fresh.append(update * cand + (1.0 - update) * before)
        pieces = fresh
        states.append(jnp.concatenate(pieces, 1).astype(jnp.bfloat16))
        stoch = samps[:, step]
    return jnp.stack(states, 1)


def on_device(
    replay_deter,
    replay_stoch,
    send_rows,
    send_counts,
    actions,
    samples,
    w_stoch,
    w_deter,
    act_table,
    w_prior,
):
    peers, cap = send_rows.shape
    slots = peers * cap
    deter = replay_deter.shape[1]
    stoch_full = lax.all_gather(w_stoch, "gy", axis=0, tiled=True)
    deter_full = lax.all_gather(w_deter, "gy", axis=1, tiled=True)
    outgoing = (jnp.arange(cap, dtype=jnp.int32)[None, :] < send_counts[0][:, None]).astype(
        jnp.int32
    )
    start = replay_deter[send_rows]
    first = replay_stoch[send_rows]
    start, first, live = (
        lax.all_to_all(start, ("gx", "gy"), split_axis=0, concat_axis=0, tiled=True),
        lax.all_to_all(first, ("gx", "gy"), split_axis=0, concat_axis=0, tiled=True),
        lax.all_to_all(outgoing, ("gx", "gy"), split_axis=0, concat_axis=0, tiled=True),
    )
    live = live.reshape(slots)
    states = imagine(
        start.reshape(slots, deter),
        first.reshape(slots, GROUPS),
        actions,
        samples,
        stoch_full,
        deter_full,
        act_table,
    )
    states = jnp.where(live[:, None, None] > 0, states, jnp.zeros_like(states))
    prior_full = lax.all_gather(w_prior, "gy", axis=0, tiled=True)
    logits = jnp.dot(
        states.reshape(slots * STEPS, deter), prior_full, preferred_element_type=jnp.float32
    )
    logits = logits.reshape(slots, STEPS, GROUPS, CLASSES)
    totals = jnp.log(jnp.sum(jnp.exp(logits), -1))
    hits = samples[..., None] == jnp.arange(CLASSES, dtype=jnp.int32)
    picked = jnp.sum(jnp.where(hits, logits, jnp.zeros_like(logits)), -1)
    log_prob = jnp.where(live[:, None, None] > 0, picked - totals, jnp.zeros_like(totals))
    return (states, log_prob)


def solution(mesh):
    in_specs = (
        P(("gx", "gy"), None),
        P(("gx", "gy"), None),
        P(("gx", "gy"), None),
        P(("gx", "gy"), None),
        P(("gx", "gy"), None),
        P(("gx", "gy"), None, None),
        P("gy", None),
        P(None, "gy", None),
        P(),
        P("gy", None),
    )
    out_specs = (P(("gx", "gy"), None, None), P(("gx", "gy"), None, None))
    return jax.shard_map(
        on_device, mesh=mesh, in_specs=in_specs, out_specs=out_specs, check_vma=False
    )
```

profile of v0, /device:TPU:0, one launch (start us, length us, event | category | flops | bytes accessed | tf_op | source)
XLA Modules:
  0.0 338.7 jit_solution(16087413320578995944)
XLA Ops:
  7.2 0.7 all-gather.8.cloned.1.call-update
  8.0 0.7 all-gather.4.cloned.1.call-update
  8.7 0.7 all-gather.6.cloned.1.call-update
  9.4 1.4 compare_convert_fusion
  10.8 7.3 %all-to-all-start = ((s32[32,1,8]{2,1,0:T(1,128)}), s32[32,1,8]{2,1,0:T(1,128)S(1)}, u32[]{:S(2)}, u32[]{:S(2)}) async-start(s32[32,1,8]{2,1,0:T(1,128)} %compare_convert_fusion), calls=%async_computation | async-start | bytes 32768 | tf_op jit(solution)/shard_map/all_to_all | solution.py:76
  18.1 0.7 compare_select_fusion
  19.0 0.9 copy.24
  19.8 0.7 gather_fusion
  20.6 0.7 reshape.433
  21.3 3.9 %all-to-all-done = s32[32,1,8]{2,1,0:T(1,128)S(1)} async-done(((s32[32,1,8]{2,1,0:T(1,128)}), s32[32,1,8]{2,1,0:T(1,128)S(1)}, u32[]{:S(2)}, u32[]{:S(2)}) %all-to-all-start) | async-done | bytes 1056 | tf_op jit(solution)/shard_map/all_to_all | solution.py:76
  25.2 2.6 all-to-all-start.1
  27.8 2.7 gather_fusion.1
  30.5 5.0 %all-to-all-done.1 = s32[32,1,256]{2,1,0:T(1,128)S(1)} async-done(((s32[32,1,256]{2,1,0:T(1,128)}), s32[32,1,256]{2,1,0:T(1,128)S(1)}, u32[]{:S(2)}, u32[]{:S(2)}) %all-to-all-start.1) | async-done | bytes 32800 | tf_op jit(solution)/shard_map/all_to_all | solution.py:75
  35.4 2.7 all-to-all-start.2
  39.0 0.7 reduce.2
  39.8 1.5 bitcast_compare_fusion
  41.3 41.9 %all-gather.8.cloned.1.call-done = bf16[2048,1024]{1,0:T(8,128)(2,1)} async-done(((bf16[256,1024]{1,0:T(8,128)(2,1)}), bf16[2048,1024]{1,0:T(8,128)(2,1)}) %all-gather.8.cloned.1.call-update) | async-done | bytes 4194320 | tf_op jit(solution)/shard_map/all_gather | solution.py:89
  83.2 6.5 %copy.26 = bf16[1024,2048]{1,0:T(8,128)(2,1)} copy(bf16[1024,2048]{0,1:T(8,128)(2,1)} %bitcast.116) | data formatting | bytes 8388608 | tf_op jit(solution)/shard_map/dot_general | solution.py:90
  89.7 116.9 %all-gather.4.cloned.1.call-done = bf16[1024,6144]{1,0:T(8,128)(2,1)} async-done(((bf16[128,6144]{1,0:T(8,128)(2,1)}), bf16[1024,6144]{1,0:T(8,128)(2,1)}) %all-gather.4.cloned.1.call-update) | async-done | bytes 12582928 | tf_op jit(solution)/shard_map/all_gather | solution.py:66
  206.6 7.0 %fusion.199 = f32[256,6144]{1,0:T(8,128)S(1)} fusion(pred[256,1024]{0,1:T(32,128)(4,1)S(1)} %get-tuple-element.50, bf16[1024,6144]{1,0:T(8,128)(2,1)} %all-gather.4.cloned.1.call-done), kind=kOutput, calls=%fused_computation.297 | convolution fusion | flops 3221225472 | bytes 19136512 | tf_op jit(solution)/shard_map/dot_general | solution.py:32
  213.6 3.7 %convolution_add_fusion.3 = f32[256,6144]{1,0:T(8,128)} fusion(f32[256,6144]{1,0:T(8,128)S(1)} %fusion.199, bf16[18,6144]{1,0:T(8,128)(2,1)S(1)} %copy-done.3, s32[256]{0:T(256)S(1)} %bitcast.122), kind=kOutput, calls=%fused_computation.5 | convolution fusion | flops 58200576 | bytes 12805120 | tf_op jit(solution)/shard_map/dot_general | solution.py:32
  217.3 3.6 %fusion.200 = f32[256,6144]{1,0:T(8,128)S(1)} fusion(pred[256,1024]{0,1:T(32,128)(4,1)S(1)} %get-tuple-element.48, bf16[1024,6144]{1,0:T(8,128)(2,1)S(1)} %bitcast.104), kind=kOutput, calls=%fused_computation.298 | convolution fusion | flops 3221225472 | bytes 19136512 | tf_op jit(solution)/shard_map/dot_general | solution.py:32
  221.0 3.6 %convolution_add_fusion.2 = f32[256,6144]{1,0:T(8,128)} fusion(f32[256,6144]{1,0:T(8,128)S(1)} %fusion.200, bf16[18,6144]{1,0:T(8,128)(2,1)S(1)} %copy-done.3, s32[256]{0:T(256)S(1)} %bitcast.121), kind=kOutput, calls=%fused_computation.4 | convolution fusion | flops 58200576 | bytes 12805120 | tf_op jit(solution)/shard_map/dot_general | solution.py:32
  224.6 47.0 %all-gather.6.cloned.1.call-done = bf16[4,512,1536]{2,1,0:T(8,128)(2,1)} async-done(((bf16[4,64,1536]{2,1,0:T(8,128)(2,1)}), bf16[4,512,1536]{2,1,0:T(8,128)(2,1)}) %all-gather.6.cloned.1.call-update) | async-done | bytes 6291472 | tf_op jit(solution)/shard_map/all_gather | solution.py:67
  271.6 2.6 convolution_add_fusion.16
  274.2 2.6 convolution_add_fusion.17
  276.8 2.0 convolution_add_fusion.18
  278.8 2.1 convolution_add_fusion.19
  281.0 2.3 convert_bitcast_fusion.11
  284.0 1.2 copy-done.7
  286.3 1.6 convert_bitcast_fusion.6
  287.9 5.6 %fusion.201 = f32[256,6144]{1,0:T(8,128)} fusion(pred[256,1024]{0,1:T(32,128)(4,1)S(1)} %copy-done.14, bf16[1024,6144]{1,0:T(8,128)(2,1)S(1)} %bitcast.106), kind=kOutput, calls=%fused_computation.299 | convolution fusion | flops 3221225472 | bytes 19136512 | tf_op jit(solution)/shard_map/dot_general | solution.py:32
  293.5 3.8 %convolution_add_fusion.1 = f32[256,6144]{1,0:T(8,128)S(1)} fusion(f32[256,6144]{1,0:T(8,128)} %fusion.201, bf16[18,6144]{1,0:T(8,128)(2,1)S(1)} %copy-done.4, s32[256]{0:T(256)S(1)} %bitcast.120), kind=kOutput, calls=%fused_computation.3 | convolution fusion | flops 58200576 | bytes 12805120 | tf_op jit(solution)/shard_map/dot_general | solution.py:32
  297.3 0.6 convolution_add_fusion.11
  297.9 1.2 convert_bitcast_fusion.3
  299.2 6.5 %fusion.202 = f32[256,6144]{1,0:T(8,128)} fusion(pred[256,1024]{0,1:T(32,128)(4,1)} %get-tuple-element.47, bf16[1024,6144]{1,0:T(8,128)(2,1)S(1)} %bitcast.106), kind=kOutput, calls=%fused_computation.300 | convolution fusion | flops 3221225472 | bytes 19136512 | tf_op jit(solution)/shard_map/dot_general | solution.py:32
  305.7 3.9 %convolution_add_fusion = f32[256,6144]{1,0:T(8,128)S(1)} fusion(f32[256,6144]{1,0:T(8,128)} %fusion.202, bf16[18,6144]{1,0:T(8,128)(2,1)S(1)} %copy-done.4, s32[256]{0:T(256)S(1)} %bitcast.119), kind=kOutput, calls=%fused_computation.2 | convolution fusion | flops 58200576 | bytes 12805120 | tf_op jit(solution)/shard_map/dot_general | solution.py:32
  309.6 0.6 convolution_add_fusion.7
  311.6 0.6 convolution_add_fusion.6
  313.3 0.6 convolution_add_fusion.12
  313.9 0.7 convert_bitcast_fusion.4
  314.6 0.6 convolution_add_fusion.9
  315.5 0.6 convolution_add_fusion.5
  316.5 0.6 convolution_add_fusion.8
  318.9 1.7 maximum_select_fusion
  320.6 5.3 %copy.27 = bf16[256,4,2048]{2,1,0:T(4,128)(2,1)} copy(bf16[256,4,2048]{2,0,1:T(8,128)(2,1)S(1)} %maximum_select_fusion) | data formatting | bytes 8388608
  325.8 5.6 %exponential_reduce_fusion = (f32[256,4,32]{0,2,1:T(8,128)S(1)}, f32[256,4,32]{0,2,1:T(8,128)S(1)}) fusion(s32[256,4,32]{0,2,1:T(8,128)S(1)} %copy-done.22, bf16[32,32,2048,1]{2,1,0,3:T(8,128)(2,1)S(1)} %bitcast.115, bf16[256,4,2048]{2,0,1:T(8,128)(2,1)S(1)} %maximum_select_fusion), kind=kOutput, calls=%fused_computation.9 | convolution fusion | flops 4299096064 | bytes 8781824 | tf_op jit(solution)/shard_map/dot_general | solution.py:90
  331.5 0.7 subtract_select_fusion
  (94 shorter events, 7.9 us)
Async XLA Ops:
  7.2 20.6 %copy-start = (f32[256,2048]{1,0:T(8,128)S(1)}, f32[256,2048]{1,0:T(8,128)}, u32[]{:S(2)}) copy-start(f32[256,2048]{1,0:T(8,128)} %param.10) | copy-start | bytes 6291460
  7.2 76.0 %all-gather.8.cloned.1.call-start = ((), (), s32[]{:S(2)}) async-start(), calls=%async_computation.5 | async-start | bytes 4718592 | tf_op jit(solution)/shard_map/all_gather | solution.py:89
  7.9 198.7 %all-gather.4.cloned.1.call-start = ((), (), s32[]{:S(2)}) async-start(), calls=%async_computation.3 | async-start | bytes 14155776 | tf_op jit(solution)/shard_map/all_gather | solution.py:66
  8.7 262.9 %all-gather.6.cloned.1.call-start = ((), (), s32[]{:S(2)}) async-start(), calls=%async_computation.4 | async-start | bytes 7077888 | tf_op jit(solution)/shard_map/all_gather | solution.py:67
  10.8 14.4 %all-to-all-start = ((s32[32,1,8]{2,1,0:T(1,128)}), s32[32,1,8]{2,1,0:T(1,128)S(1)}, u32[]{:S(2)}, u32[]{:S(2)}) async-start(s32[32,1,8]{2,1,0:T(1,128)} %compare_convert_fusion), calls=%async_computation | async-start | bytes 32768 | tf_op jit(solution)/shard_map/all_to_all | solution.py:76
  25.2 10.2 %all-to-all-start.1 = ((s32[32,1,256]{2,1,0:T(1,128)}), s32[32,1,256]{2,1,0:T(1,128)S(1)}, u32[]{:S(2)}, u32[]{:S(2)}) async-start(s32[32,1,256]{2,1,0:T(1,128)} %reshape.433), calls=%async_computation.1 | async-start | bytes 65536 | tf_op jit(solution)/shard_map/all_to_all | solution.py:75
  30.5 7.8 %copy-start.23 = (s32[256,4]{0,1:T(4,128)S(1)}, s32[256,4]{0,1:T(4,128)}, u32[]{:S(2)}) copy-start(s32[256,4]{0,1:T(4,128)} %param.14) | copy-start | bytes 12292
  30.5 7.8 %copy-start.22 = (s32[256,4,32]{0,2,1:T(8,128)S(1)}, s32[256,4,32]{0,2,1:T(8,128)}, u32[]{:S(2)}) copy-start(s32[256,4,32]{0,2,1:T(8,128)} %param.15) | copy-start | bytes 393220
  35.4 189.2 %all-to-all-start.2 = ((f32[32,8,2048]{2,1,0:T(8,128)}), f32[32,8,2048]{2,1,0:T(8,128)S(1)}, u32[]{:S(2)}, u32[]{:S(2)}) async-start(f32[32,8,2048]{2,1,0:T(8,128)} %bitcast.114), calls=%async_computation.2 | async-start | bytes 4194304 | tf_op jit(solution)/shard_map/all_to_all | solution.py:74
  206.6 7.0 %copy-start.3 = (bf16[18,6144]{1,0:T(8,128)(2,1)S(1)}, bf16[18,6144]{1,0:T(8,128)(2,1)}, u32[]{:S(2)}) copy-start(bf16[18,6144]{1,0:T(8,128)(2,1)} %param.18) | copy-start | bytes 663556
  206.6 10.7 %slice-start = ((s8[12582912]{0:T(1024)(128)(4,1)}), s8[4194304]{0:T(1024)(128)(4,1)S(1)}, s32[]{:S(2)}) async-start(s8[12582912]{0:T(1024)(128)(4,1)} %bitcast.103), calls=%async_computation.6 | async-start | bytes 8388608
  206.6 10.7 %slice-start.1 = ((s8[12582912]{0:T(1024)(128)(4,1)}), s8[4194304]{0:T(1024)(128)(4,1)S(1)}, s32[]{:S(2)}) async-start(s8[12582912]{0:T(1024)(128)(4,1)} %bitcast.103), calls=%async_computation.7 | async-start | bytes 8388608
  213.6 3.7 %slice-start.2 = ((s8[12582912]{0:T(1024)(128)(4,1)}), s8[4194304]{0:T(1024)(128)(4,1)S(1)}, s32[]{:S(2)}) async-start(s8[12582912]{0:T(1024)(128)(4,1)} %bitcast.103), calls=%async_computation.8 | async-start | bytes 8388608
  271.6 5.2 %copy-start.2 = (bf16[4,512,1536]{2,1,0:T(8,128)(2,1)S(1)}, bf16[4,512,1536]{2,1,0:T(8,128)(2,1)}, u32[]{:S(2)}) copy-start(bf16[4,512,1536]{2,1,0:T(8,128)(2,1)} %all-gather.6.cloned.1.call-done) | copy-start | bytes 18874372
  274.2 9.1 %slice-start.6 = ((s8[6291456]{0:T(1024)(128)(4,1)}), s8[4194304]{0:T(1024)(128)(4,1)S(1)}, s32[]{:S(2)}) async-start(s8[6291456]{0:T(1024)(128)(4,1)} %bitcast.107), calls=%async_computation.12 | async-start | bytes 8388608
  278.8 4.5 %slice-start.7 = ((s8[6291456]{0:T(1024)(128)(4,1)}), s8[2097152]{0:T(1024)(128)(4,1)S(1)}, s32[]{:S(2)}) async-start(s8[6291456]{0:T(1024)(128)(4,1)} %bitcast.107), calls=%async_computation.13 | async-start | bytes 4194304
  280.9 6.9 %slice-start.3 = ((s8[12582912]{0:T(1024)(128)(4,1)}), s8[4194304]{0:T(1024)(128)(4,1)S(1)}, s32[]{:S(2)}) async-start(s8[12582912]{0:T(1024)(128)(4,1)} %bitcast.105), calls=%async_computation.9 | async-start | bytes 8388608
  281.0 6.9 %slice-start.4 = ((s8[12582912]{0:T(1024)(128)(4,1)}), s8[4194304]{0:T(1024)(128)(4,1)S(1)}, s32[]{:S(2)}) async-start(s8[12582912]{0:T(1024)(128)(4,1)} %bitcast.105), calls=%async_computation.10 | async-start | bytes 8388608
  283.2 0.8 copy-start.8
  283.2 2.0 copy-start.7
  285.2 1.0 copy-start.9
  285.2 2.6 slice-start.5
  286.3 1.6 copy-start.14
  287.9 5.6 %copy-start.4 = (bf16[18,6144]{1,0:T(8,128)(2,1)S(1)}, bf16[18,6144]{1,0:T(8,128)(2,1)}, u32[]{:S(2)}) copy-start(bf16[18,6144]{1,0:T(8,128)(2,1)} %param.18) | copy-start | bytes 663556
  293.5 3.9 %copy-start.12 = (f32[256,512]{1,0:T(8,128)S(1)}, f32[256,512]{1,0:T(8,128)}, u32[]{:S(2)}) copy-start(f32[256,512]{1,0:T(8,128)} %get-tuple-element.54) | copy-start | bytes 1572868
  305.7 3.9 %copy-start.10 = (f32[256,512]{1,0:T(8,128)S(1)}, f32[256,512]{1,0:T(8,128)}, u32[]{:S(2)}) copy-start(f32[256,512]{1,0:T(8,128)} %get-tuple-element.27) | copy-start | bytes 1572868
  309.6 1.0 copy-start.11
  311.6 1.0 copy-start.5
  312.2 1.1 copy-start.6
  317.5 1.0 copy-start.15
  317.5 1.0 copy-start.16
  317.5 1.1 copy-start.17
  317.5 1.2 copy-start.18
  317.5 1.2 copy-start.19
  317.5 1.3 copy-start.20
  317.5 1.4 copy-start.21
  320.6 5.3 %copy-start.13 = (bf16[1024,2048]{1,0:T(8,128)(2,1)S(1)}, bf16[1024,2048]{1,0:T(8,128)(2,1)}, u32[]{:S(2)}) copy-start(bf16[1024,2048]{1,0:T(8,128)(2,1)} %copy.26) | copy-start | bytes 12582916
  325.8 6.3 %copy-start.1 = (f32[256,2048]{1,0:T(8,128)S(1)}, f32[256,2048]{1,0:T(8,128)}, u32[]{:S(2)}) copy-start(f32[256,2048]{1,0:T(8,128)} %param.10) | copy-start | bytes 6291460
Sparse Core Ops, SparseCore 0:
  9.6 73.5 all-gather.7
  84.8 121.7 all-gather.3
  208.2 63.3 all-gather.5
where the time goes:
time: 339 us
  waiting for transfers between devices  217 us (64%)
  matrix products  59.7 us (18%)
  local copies, waits for them, and re-layouts  20.3 us (6%)
  other arithmetic  15 us (4%)
  between operations  14.3 us (4%)
  starting transfers between devices  12.7 us (4%)
    all_gather x1, waiting for transfers between devices, on_device(): stoch_full = lax.all_gather(w_stoch, 'gy', axis=0, tiled=True)  117 us
    all_gather x1, waiting for transfers between devices, on_device(): deter_full = lax.all_gather(w_deter, 'gy', axis=1, tiled=True)  47 us
    all_gather x1, waiting for transfers between devices, on_device(): prior_full = lax.all_gather(w_prior, 'gy', axis=0, tiled=True)  41.9 us
    dot_general x4, matrix products, imagine(): jnp.dot(onehot, stoch_full, preferred_element_type=jnp.float32)  22.7 us
    dot_general x16, matrix products, imagine(): jnp.dot(before.astype(jnp.bfloat16), deter_full[b], preferred_element_typ...  16.3 us
    dot_general x4, matrix products, imagine(): jnp.dot(act_hot, act_table, preferred_element_type=jnp.float32)  15 us
    unnamed x68, local copies, waits for them, and re-layouts  9.44 us
    concatenate x11, other arithmetic, imagine(): states.append(jnp.concatenate(pieces, 1).astype(jnp.bfloat16))  8.3 us
  transfers between devices with their start and end apart: 6, of which 5 were waited for; matrix products, arithmetic and copies ran while one was open for 10% of the time, Pallas kernels for 0%

commit v1 on v0

--- a/solution.py
+++ b/solution.py
@@ -2,6 +2,7 @@
 import jax.numpy as jnp
 from jax import lax
 from jax.sharding import PartitionSpec as P
+from jax.lax import all_gather
 
 GROUPS = 32
 CLASSES = 32
@@ -64,7 +65,12 @@
     slots = peers * cap
     deter = replay_deter.shape[1]
     stoch_full = lax.all_gather(w_stoch, "gy", axis=0, tiled=True)
-    deter_full = lax.all_gather(w_deter, "gy", axis=1, tiled=True)
+
+    def create_the_results(original, mesh_name):
+        r2 = all_gather(original, mesh_name)
+        return jnp.concatenate(r2, 1)
+
+    deter_full = create_the_results(w_deter, "gy")
     outgoing = (jnp.arange(cap, dtype=jnp.int32)[None, :] < send_counts[0][:, None]).astype(
         jnp.int32
     )

time: 339 us -> 362 us (1.068)
  waiting for transfers between devices: 217 us -> 232 us
  local copies, waits for them, and re-layouts: 20.3 us -> 24.7 us
    all_gather x1, waiting for transfers between devices: 47 us -> 66.1 us  [create_the_results(): r2 = all_gather(original, mesh_name)]
    slice x0 -> x1, local copies, waits for them, and re-layouts: none -> 5.09 us  [imagine(): deter_full[b]]
    all_gather x1, waiting for transfers between devices: 117 us -> 112 us  [on_device(): stoch_full = lax.all_gather(w_stoch, 'gy', axis=0, tiled=True)]
    unnamed x68 -> x56, local copies, waits for them, and re-layouts: 9.44 us -> 8.74 us
  transfers between devices with their start and end apart: 6 -> 6, of which waited for: 5 -> 5; matrix products, arithmetic and copies ran while one was open for 10% -> 8% of each run, Pallas kernels for 0% -> 0%
where the time goes in v1:
time: 362 us; the launch traced here: 361 us
  waiting for transfers between devices  232 us (64%)
  matrix products  60.2 us (17%)
  local copies, waits for them, and re-layouts  24.7 us (7%)
  other arithmetic  16.2 us (4%)
  between operations  14.3 us (4%)
  starting transfers between devices  13.6 us (4%)
    all_gather x1, waiting for transfers between devices, on_device(): stoch_full = lax.all_gather(w_stoch, 'gy', axis=0, tiled=True)  112 us
    all_gather x1, waiting for transfers between devices, create_the_results(): r2 = all_gather(original, mesh_name)  66.1 us
    all_gather x1, waiting for transfers between devices, on_device(): prior_full = lax.all_gather(w_prior, 'gy', axis=0, tiled=True)  41.5 us
    dot_general x4, matrix products, imagine(): jnp.dot(onehot, stoch_full, preferred_element_type=jnp.float32)  25.6 us
    dot_general x16, matrix products, imagine(): jnp.dot(before.astype(jnp.bfloat16), deter_full[b], preferred_element_typ...  16.5 us
    dot_general x4, matrix products, imagine(): jnp.dot(act_hot, act_table, preferred_element_type=jnp.float32)  12.3 us
    concatenate x11, other arithmetic, imagine(): states.append(jnp.concatenate(pieces, 1).astype(jnp.bfloat16))  11.1 us
    unnamed x56, local copies, waits for them, and re-layouts  8.74 us
  transfers between devices with their start and end apart: 6, of which 5 were waited for; matrix products, arithmetic and copies ran while one was open for 8% of the time, Pallas kernels for 0%

profile of v1, /device:TPU:0, one launch (start us, length us, event | category | flops | bytes accessed | tf_op | source)
XLA Modules:
  0.0 361.0 jit_solution(18183628347344249325)
XLA Ops:
  7.3 0.7 all-gather.7.cloned.1.call-update
  8.0 0.7 all-gather.9.cloned.1.call-update
  8.7 0.7 all-gather.5.cloned.1.call-update
  9.4 0.7 compare_convert_fusion
  10.1 7.3 %all-to-all-start = ((s32[32,1,8]{2,1,0:T(1,128)}), s32[32,1,8]{2,1,0:T(1,128)S(1)}, u32[]{:S(2)}, u32[]{:S(2)}) async-start(s32[32,1,8]{2,1,0:T(1,128)} %compare_convert_fusion), calls=%async_computation | async-start | bytes 32768 | tf_op jit(solution)/shard_map/all_to_all | solution.py:82
  17.8 0.7 gather_fusion
  18.5 0.7 reshape.447
  19.3 5.3 %all-to-all-done = s32[32,1,8]{2,1,0:T(1,128)S(1)} async-done(((s32[32,1,8]{2,1,0:T(1,128)}), s32[32,1,8]{2,1,0:T(1,128)S(1)}, u32[]{:S(2)}, u32[]{:S(2)}) %all-to-all-start) | async-done | bytes 1056 | tf_op jit(solution)/shard_map/all_to_all | solution.py:82
  24.6 2.6 all-to-all-start.1
  27.2 2.7 gather_fusion.1
  29.8 5.0 %all-to-all-done.1 = s32[32,1,256]{2,1,0:T(1,128)S(1)} async-done(((s32[32,1,256]{2,1,0:T(1,128)}), s32[32,1,256]{2,1,0:T(1,128)S(1)}, u32[]{:S(2)}, u32[]{:S(2)}) %all-to-all-start.1) | async-done | bytes 32800 | tf_op jit(solution)/shard_map/all_to_all | solution.py:81
  34.8 3.6 all-to-all-start.2
  39.2 0.7 reduce.2
  40.1 1.5 bitcast_compare_fusion
  41.6 41.5 %all-gather.7.cloned.1.call-done = bf16[2048,1024]{1,0:T(8,128)(2,1)} async-done(((bf16[256,1024]{1,0:T(8,128)(2,1)}), bf16[2048,1024]{1,0:T(8,128)(2,1)}) %all-gather.7.cloned.1.call-update) | async-done | bytes 4194320 | tf_op jit(solution)/shard_map/all_gather | solution.py:95
  83.1 6.6 %copy.26 = bf16[1024,2048]{1,0:T(8,128)(2,1)} copy(bf16[1024,2048]{0,1:T(8,128)(2,1)} %bitcast.123) | data formatting | bytes 8388608 | tf_op jit(solution)/shard_map/dot_general | solution.py:96
  89.7 66.1 %all-gather.9.cloned.1.call-done = bf16[32,64,1536]{2,1,0:T(8,128)(2,1)} async-done(((bf16[4,64,1536]{2,1,0:T(8,128)(2,1)}), bf16[32,64,1536]{2,1,0:T(8,128)(2,1)}) %all-gather.9.cloned.1.call-update) | async-done | bytes 6291472 | tf_op jit(solution)/shard_map/all_gather | solution.py:70
  155.8 5.1 %fusion.198 = (bf16[1,8,64,1536]{3,2,0,1:T(8,128)(2,1)}, bf16[1,8,64,1536]{3,2,0,1:T(8,128)(2,1)S(1)}, bf16[1,8,64,1536]{3,2,0,1:T(8,128)(2,1)}, bf16[1,8,64,1536]{3,2,0,1:T(8,128)(2,1)}) fusion(bf16[4,8,64,1536]{3,2,0,1:T(8,128)(2,1)} %bitcast.121), kind=kLoop, calls=%fused_computation.292 | loop fusion | bytes 12582912 | tf_op jit(solution)/shard_map/slice | solution.py:40
  160.9 111.9 %all-gather.5.cloned.1.call-done = bf16[1024,6144]{1,0:T(8,128)(2,1)} async-done(((bf16[128,6144]{1,0:T(8,128)(2,1)}), bf16[1024,6144]{1,0:T(8,128)(2,1)}) %all-gather.5.cloned.1.call-update) | async-done | bytes 12582928 | tf_op jit(solution)/shard_map/all_gather | solution.py:67
  272.8 6.7 %fusion.200 = f32[256,6144]{1,0:T(8,128)S(1)} fusion(pred[256,1024]{0,1:T(32,128)(4,1)S(1)} %get-tuple-element.54, bf16[1024,6144]{1,0:T(8,128)(2,1)} %all-gather.5.cloned.1.call-done), kind=kOutput, calls=%fused_computation.294 | convolution fusion | flops 3221225472 | bytes 19136512 | tf_op jit(solution)/shard_map/dot_general | solution.py:33
  279.6 3.7 %convolution_add_fusion.3 = f32[256,6144]{1,0:T(8,128)} fusion(f32[256,6144]{1,0:T(8,128)S(1)} %fusion.200, bf16[18,6144]{1,0:T(8,128)(2,1)S(1)} %copy-done.6, s32[256]{0:T(256)S(1)} %bitcast.129), kind=kOutput, calls=%fused_computation.5 | convolution fusion | flops 58200576 | bytes 12805120 | tf_op jit(solution)/shard_map/dot_general | solution.py:33
  283.3 2.3 convolution_add_fusion.16
  285.6 2.7 convolution_add_fusion.17
  288.5 1.7 convolution_add_fusion.18
  290.2 2.8 convolution_add_fusion.19
  293.0 6.7 %fusion.201 = f32[256,6144]{1,0:T(8,128)S(1)} fusion(pred[256,1024]{0,1:T(32,128)(4,1)S(1)} %get-tuple-element.52, bf16[1024,6144]{1,0:T(8,128)(2,1)} %all-gather.5.cloned.1.call-done), kind=kOutput, calls=%fused_computation.295 | convolution fusion | flops 3221225472 | bytes 19136512 | tf_op jit(solution)/shard_map/dot_general | solution.py:33
  299.6 1.0 convolution_add_fusion.2
  300.7 4.4 %convert_bitcast_fusion.11 = (bf16[256,1,512]{2,0,1:T(8,128)(2,1)}, f32[256,512]{1,0:T(8,128)S(1)}, bf16[256,1,512]{2,0,1:T(8,128)(2,1)}, f32[256,512]{1,0:T(8,1...) fusion(f32[256,2048]{1,0:T(8,128)} %bitcast.6, ...), kind=kLoop, calls=%fused_computation.279 | loop fusion | flops 6815744 | bytes 11534336 | tf_op jit(solution)/shard_map/concatenate | solution.py:47
  305.7 0.6 convolution_add_fusion.15
  306.2 1.4 convert_bitcast_fusion.6
  308.4 5.6 %fusion.202 = f32[256,6144]{1,0:T(8,128)} fusion(pred[256,1024]{0,1:T(32,128)(4,1)S(1)} %copy-done.10, bf16[1024,6144]{1,0:T(8,128)(2,1)S(1)} %bitcast.103), kind=kOutput, calls=%fused_computation.296 | convolution fusion | flops 3221225472 | bytes 19136512 | tf_op jit(solution)/shard_map/dot_general | solution.py:33
  314.0 3.8 %convolution_add_fusion.1 = f32[256,6144]{1,0:T(8,128)S(1)} fusion(f32[256,6144]{1,0:T(8,128)} %fusion.202, bf16[18,6144]{1,0:T(8,128)(2,1)S(1)} %copy-done.6, s32[256]{0:T(256)S(1)} %bitcast.127), kind=kOutput, calls=%fused_computation.3 | convolution fusion | flops 58200576 | bytes 12805120 | tf_op jit(solution)/shard_map/dot_general | solution.py:33
  318.4 2.1 convert_bitcast_fusion.3
  320.5 6.6 %fusion.203 = f32[256,6144]{1,0:T(8,128)} fusion(pred[256,1024]{0,1:T(32,128)(4,1)} %get-tuple-element.51, bf16[1024,6144]{1,0:T(8,128)(2,1)S(1)} %bitcast.103), kind=kOutput, calls=%fused_computation.297 | convolution fusion | flops 3221225472 | bytes 19136512 | tf_op jit(solution)/shard_map/dot_general | solution.py:33
  327.1 3.8 %convolution_add_fusion = f32[256,6144]{1,0:T(8,128)S(1)} fusion(f32[256,6144]{1,0:T(8,128)} %fusion.203, bf16[18,6144]{1,0:T(8,128)(2,1)S(1)} %copy-done.6, s32[256]{0:T(256)S(1)} %bitcast.126), kind=kOutput, calls=%fused_computation.2 | convolution fusion | flops 58200576 | bytes 12805120 | tf_op jit(solution)/shard_map/dot_general | solution.py:33
  330.9 0.6 convolution_add_fusion.7
  331.9 0.7 copy-done.7
  332.6 0.6 convolution_add_fusion.10
  333.5 0.6 convolution_add_fusion.6
  335.6 0.7 convert_bitcast_fusion.4
  336.3 0.6 convolution_add_fusion.9
  337.3 0.6 convolution_add_fusion.5
  338.3 0.6 convolution_add_fusion.8
  339.2 0.6 convolution_add_fusion.4
  341.2 1.4 maximum_select_fusion
  342.7 5.3 %copy.27 = bf16[256,4,2048]{2,1,0:T(4,128)(2,1)} copy(bf16[256,4,2048]{2,0,1:T(8,128)(2,1)S(1)} %maximum_select_fusion) | data formatting | bytes 8388608
  347.9 5.8 %exponential_reduce_fusion = (f32[256,4,32]{0,2,1:T(8,128)S(1)}, f32[256,4,32]{0,2,1:T(8,128)S(1)}) fusion(s32[256,4,32]{0,2,1:T(8,128)S(1)} %copy-done.18, bf16[32,32,2048,1]{2,1,0,3:T(8,128)(2,1)S(1)} %bitcast.122, bf16[256,4,2048]{2,0,1:T(8,128)(2,1)S(1)} %maximum_select_fusion), kind=kOutput, calls=%fused_computation.9 | convolution fusion | flops 4299096064 | bytes 8781824 | tf_op jit(solution)/shard_map/dot_general | solution.py:96
  353.8 0.7 subtract_select_fusion
  (81 shorter events, 8.0 us)
Async XLA Ops:
  7.2 20.0 %copy-start = (f32[256,2048]{1,0:T(8,128)S(1)}, f32[256,2048]{1,0:T(8,128)}, u32[]{:S(2)}) copy-start(f32[256,2048]{1,0:T(8,128)} %param.10) | copy-start | bytes 6291460
  7.2 2.3 copy-start.22
  7.2 10.3 %copy-start.20 = (s32[32,8]{0,1:T(8,128)S(1)}, s32[32,8]{0,1:T(8,128)}, u32[]{:S(2)}) copy-start(s32[32,8]{0,1:T(8,128)} %param.12) | copy-start | bytes 3076
  7.2 10.5 %copy-start.19 = (s32[256,32]{0,1:T(8,128)S(1)}, s32[256,32]{0,1:T(8,128)}, u32[]{:S(2)}) copy-start(s32[256,32]{0,1:T(8,128)} %param.11) | copy-start | bytes 98308
  7.2 75.9 %all-gather.7.cloned.1.call-start = ((), (), s32[]{:S(2)}) async-start(), calls=%async_computation.4 | async-start | bytes 4718592 | tf_op jit(solution)/shard_map/all_gather | solution.py:95
  7.9 147.9 %all-gather.9.cloned.1.call-start = ((), (), s32[]{:S(2)}) async-start(), calls=%async_computation.5 | async-start | bytes 7077888 | tf_op jit(solution)/shard_map/all_gather | solution.py:70
  8.7 264.1 %all-gather.5.cloned.1.call-start = ((), (), s32[]{:S(2)}) async-start(), calls=%async_computation.3 | async-start | bytes 14155776 | tf_op jit(solution)/shard_map/all_gather | solution.py:67
  10.1 14.4 %all-to-all-start = ((s32[32,1,8]{2,1,0:T(1,128)}), s32[32,1,8]{2,1,0:T(1,128)S(1)}, u32[]{:S(2)}, u32[]{:S(2)}) async-start(s32[32,1,8]{2,1,0:T(1,128)} %compare_convert_fusion), calls=%async_computation | async-start | bytes 32768 | tf_op jit(solution)/shard_map/all_to_all | solution.py:82
  24.6 10.2 %all-to-all-start.1 = ((s32[32,1,256]{2,1,0:T(1,128)}), s32[32,1,256]{2,1,0:T(1,128)S(1)}, u32[]{:S(2)}, u32[]{:S(2)}) async-start(s32[32,1,256]{2,1,0:T(1,128)} %reshape.447), calls=%async_computation.1 | async-start | bytes 65536 | tf_op jit(solution)/shard_map/all_to_all | solution.py:81
  34.8 3.7 %copy-start.21 = (s32[256,4]{0,1:T(4,128)S(1)}, s32[256,4]{0,1:T(4,128)}, u32[]{:S(2)}) copy-start(s32[256,4]{0,1:T(4,128)} %param.14) | copy-start | bytes 12292
  34.8 3.7 %copy-start.18 = (s32[256,4,32]{0,2,1:T(8,128)S(1)}, s32[256,4,32]{0,2,1:T(8,128)}, u32[]{:S(2)}) copy-start(s32[256,4,32]{0,2,1:T(8,128)} %param.15) | copy-start | bytes 393220
  34.8 248.5 %all-to-all-start.2 = ((f32[32,8,2048]{2,1,0:T(8,128)}), f32[32,8,2048]{2,1,0:T(8,128)}, u32[]{:S(2)}, u32[]{:S(2)}) async-start(f32[32,8,2048]{2,1,0:T(8,128)} %bitcast.120), calls=%async_computation.2 | async-start | bytes 4194304 | tf_op jit(solution)/shard_map/all_to_all | solution.py:80
  272.8 6.7 %copy-start.6 = (bf16[18,6144]{1,0:T(8,128)(2,1)S(1)}, bf16[18,6144]{1,0:T(8,128)(2,1)}, u32[]{:S(2)}) copy-start(bf16[18,6144]{1,0:T(8,128)(2,1)} %param.18) | copy-start | bytes 663556
  283.3 2.3 copy-start.2
  283.3 5.1 %copy-start.5 = (f32[256,6144]{1,0:T(8,128)S(1)}, f32[256,6144]{1,0:T(8,128)}, u32[]{:S(2)}) copy-start(f32[256,6144]{1,0:T(8,128)} %convolution_add_fusion.3) | copy-start | bytes 18874372
  285.6 2.9 copy-start.3
  288.5 1.7 copy-start.4
  300.7 7.0 %slice-start = ((s8[12582912]{0:T(1024)(128)(4,1)}), s8[4194304]{0:T(1024)(128)(4,1)S(1)}, s32[]{:S(2)}) async-start(s8[12582912]{0:T(1024)(128)(4,1)} %bitcast.102), calls=%async_computation.6 | async-start | bytes 8388608
  300.7 7.0 %slice-start.1 = ((s8[12582912]{0:T(1024)(128)(4,1)}), s8[4194304]{0:T(1024)(128)(4,1)S(1)}, s32[]{:S(2)}) async-start(s8[12582912]{0:T(1024)(128)(4,1)} %bitcast.102), calls=%async_computation.7 | async-start | bytes 8388608
  305.6 2.6 slice-start.2
  306.2 2.1 copy-start.10
  307.6 10.2 %copy-start.8 = (f32[256,512]{1,0:T(8,128)}, f32[256,512]{1,0:T(8,128)S(1)}, u32[]{:S(2)}) copy-start(f32[256,512]{1,0:T(8,128)S(1)} %get-tuple-element.58) | copy-start | bytes 1572868
  331.5 1.0 copy-start.7
  339.8 1.0 copy-start.11
  339.8 1.0 copy-start.12
  339.8 1.1 copy-start.13
  339.8 1.2 copy-start.14
  339.9 1.2 copy-start.15
  339.9 1.3 copy-start.16
  339.9 1.4 copy-start.17
  342.7 5.3 %copy-start.9 = (bf16[1024,2048]{1,0:T(8,128)(2,1)S(1)}, bf16[1024,2048]{1,0:T(8,128)(2,1)}, u32[]{:S(2)}) copy-start(bf16[1024,2048]{1,0:T(8,128)(2,1)} %copy.26) | copy-start | bytes 12582916
  347.9 6.5 %copy-start.1 = (f32[256,2048]{1,0:T(8,128)S(1)}, f32[256,2048]{1,0:T(8,128)}, u32[]{:S(2)}) copy-start(f32[256,2048]{1,0:T(8,128)} %param.10) | copy-start | bytes 6291460
Sparse Core Ops, SparseCore 0:
  9.6 73.4 all-gather.6
  84.8 71.0 all-gather.8
  157.4 115.3 all-gather.4
